TPU v7x, 128 devices: a whole 4x4x4 slice. The times are simulated.
128 devices in a mesh: section: 4 (over z), dp: 8 (over y, core), mp: 4 (over x).
Axes of the slice: x: 4, y: 4, z: 4, core: 2. Of those that a mesh axis runs over, the one named last changes fastest.
Arguments:
- text: bfloat16 [4, 4096, 4096], P('section', ('dp', 'mp')), may hold values from -6 to 6
- patches: bfloat16 [16384, 1024], P(('section', 'dp')), may hold values from -6 to 6
- segments: int32 [4, 8, 512], P('section', 'dp'), may hold values from 0 to 3, never falling along the last dimension, each value on 1 to 256 neighbouring positions
- loss_mask: int32 [4, 4096], P('section', ('dp', 'mp')), may hold values from 0 to 1, as said below
- tile_batch: int32 [8, 8], P('dp'), may hold values from 0 to 3, as said below
- tile_offset: int32 [8, 8], P('dp'), may hold values from 0 to 448, as said below
- attn_gain: float32 [4, 4096], P('section'), may hold values from 0.5 to 2
- w_query: bfloat16 [4, 4096, 2048], P('section', None, 'mp'), may hold values from -0.09375 to 0.09375
- w_kv: bfloat16 [4, 2, 4096, 512], P('section', None, None, 'mp'), may hold values from -0.09375 to 0.09375
- w_out: bfloat16 [4, 2048, 4096], P('section', 'mp'), may hold values from -0.125 to 0.125
- vis_gain: float32 [2, 1024], replicated, may hold values from 0.5 to 2
- vis_bias: float32 [2, 1024], replicated, may hold values from -3 to 3
- v_qkv: bfloat16 [3, 1024, 1024], P(None, ('section', 'dp'), 'mp'), may hold values from -0.1875 to 0.1875
- v_out: bfloat16 [1024, 1024], P('mp', ('section', 'dp')), may hold values from -0.1875 to 0.1875
- v_up: bfloat16 [1024, 4096], P(('section', 'dp'), 'mp'), may hold values from -0.1875 to 0.1875
- v_down: bfloat16 [4096, 1024], P('mp', ('section', 'dp')), may hold values from -0.09375 to 0.09375
- v_proj: bfloat16 [4096, 4096], P(('section', 'dp'), 'mp'), may hold values from -0.09375 to 0.09375
Outputs:
- hidden: bfloat16 [4, 4096, 4096], P('section', ('dp', 'mp'))
- token_weight: float32 [4, 4096], P('section', ('dp', 'mp'))
Inputs may be any that keep to these rules, and one draw needn't show every extreme that they name: `tile_batch`: in every data-parallel index, the 2 tiles of each section index go 1 to each of two different micro-batches; one micro-batch receives 1 tiles from every section index. `tile_offset`: offsets are multiples of 64; the runs of one sequence never intersect. `loss_mask`: the first position of every sequence is a one.
All inputs are finite; a program needn't handle non-finite values.
Results may differ from a plain program's by a relative error of at most 0.025.
Values may be sent and summed in bfloat16 or wider, within the bound.
No kernel may reach another device: no remote copies, remote signals or barrier semaphores. Data moves between devices by JAX's collectives and lax.ppermute only.
A program may use at most 192 MiB of HBM per device.

v0:
```python
import jax
import jax.numpy as jnp
from jax import lax
from jax.sharding import Mesh
from jax.sharding import PartitionSpec as P

HD = 128
VHD = 64
GRID = 16
PATCH = 256
POOL = 64
SECTION_DP = ("section", "dp_0", "dp_1")
SECTION_DP_MP = ("section", "dp_0", "dp_1", "mp")
DP = ("dp_0", "dp_1")
DP_MP = ("dp_0", "dp_1", "mp")


EPS = 1e-05
ROPE_BASE = 500000.0
BLOCKED = -1e30


def copy_for_each(array, axis):
    copies = jnp.broadcast_to(array, (lax.axis_size(axis), *array.shape))
    return lax.all_to_all(copies, axis, split_axis=0, concat_axis=0, tiled=True)


def over_copies(array, axis):
    everything = copy_for_each(array, axis)
    return jnp.sum(everything.astype(jnp.float32), axis=0)


def laid_out(tiles, dim):
    lengths = list(tiles.shape[1:])
    lengths[dim] *= tiles.shape[0]
    return jnp.moveaxis(tiles, 0, dim).reshape(lengths)


def one_gather(arrays, axis, dims):
    flat = jnp.concatenate([a.reshape(-1) for a in arrays])
    lines, at, done = (lax.all_gather(flat, axis), 0, [])
    for a, dim in zip(arrays, dims):
        tiles = lines[:, at : at + a.size].reshape(-1, *a.shape)
        done.append(laid_out(tiles, dim))
        at += a.size
    return tuple(done)


def shifted(value, axis, steps):
    count = lax.axis_size(axis)
    pairs = [(source, (source + steps) % count) for source in range(count)]
    return lax.ppermute(value, axis, pairs)


def over_axes(array, axes):
    for axis in axes:
        array = lax.psum(array, axis)
    return array


def layer_norm(values, gain, bias):
    wide = values.astype(jnp.float32)
    center = wide - jnp.mean(wide, axis=-1, keepdims=True)
    spread = jnp.mean(center * center, axis=-1, keepdims=True)
    return (center * lax.rsqrt(spread + EPS) * gain + bias).astype(jnp.bfloat16)


def rms_norm(values, gain):
    wide = values.astype(jnp.float32)
    power = jnp.mean(wide * wide, axis=-1, keepdims=True)
    return (wide * lax.rsqrt(power + EPS) * gain).astype(jnp.bfloat16)


def rotate(values, positions):
    half_width = values.shape[-1] // 2
    freqs = ROPE_BASE ** (-2.0 * jnp.arange(half_width, dtype=jnp.float32) / values.shape[-1])
    angles = positions.astype(jnp.float32)[:, None] * freqs[None, :]
    cosine = jnp.cos(angles)[:, None, :]
    sinus_part = jnp.sin(angles)[:, None, :]
    first_half = values[..., :half_width]
    second_half = values[..., half_width:]
    return jnp.concatenate(
        [
            first_half * cosine - second_half * sinus_part,
            second_half * cosine + first_half * sinus_part,
        ],
        axis=-1,
    )


def pixel_shuffle(states):
    tile_count = states.shape[0] // PATCH
    side_half = GRID // 2
    width = states.shape[1]
    arranged = states.reshape(tile_count, side_half, 2, side_half, 2, width)
    return arranged.transpose(0, 1, 3, 2, 4, 5).reshape(
        tile_count * side_half * side_half, 4 * width
    )


def block_sum(partial_value):
    return over_copies(partial_value.astype(jnp.bfloat16), "mp").astype(jnp.float32)


def encode_tiles(patches, vis_gain, vis_bias, qkv_full, out_full, up_full, down_full, proj_full):
    tile_count = patches.shape[0] // PATCH
    local_width = qkv_full.shape[2]
    head_count = local_width // VHD
    normed = layer_norm(patches, vis_gain[0], vis_bias[0])
    projected = [
        jnp.dot(normed, qkv_full[index], preferred_element_type=jnp.float32)
        .astype(jnp.bfloat16)
        .reshape(tile_count, PATCH, head_count, VHD)
        for index in range(3)
    ]
    scores = jnp.einsum(
        "tqhd,tkhd->thqk", projected[0], projected[1], preferred_element_type=jnp.float32
    ) * VHD ** (-0.5)
    probs = jax.nn.softmax(scores, axis=-1).astype(jnp.bfloat16)
    mixed = (
        jnp.einsum("thqk,tkhd->tqhd", probs, projected[2], preferred_element_type=jnp.float32)
        .astype(jnp.bfloat16)
        .reshape(tile_count * PATCH, local_width)
    )
    attended = block_sum(jnp.dot(mixed, out_full, preferred_element_type=jnp.float32))
    residual = (patches.astype(jnp.float32) + attended).astype(jnp.bfloat16)
    normed_two = layer_norm(residual, vis_gain[1], vis_bias[1])
    inner = jax.nn.gelu(
        jnp.dot(normed_two, up_full, preferred_element_type=jnp.float32), approximate=False
    ).astype(jnp.bfloat16)
    fed = block_sum(jnp.dot(inner, down_full, preferred_element_type=jnp.float32))
    states = (residual.astype(jnp.float32) + fed).astype(jnp.bfloat16)
    return jnp.dot(pixel_shuffle(states), proj_full, preferred_element_type=jnp.float32).astype(
        jnp.bfloat16
    )


def decoder_layer(active, state, segment_ids, gain, w_query, w_kv, w_out):
    normed = rms_norm(state, gain)
    query_width = w_query.shape[1]
    pair_width = w_kv.shape[2]
    joined_width = query_width + 2 * pair_width
    model_width = w_out.shape[1]
    piece = lax.all_gather(normed, "mp", axis=0, tiled=True)
    row_count = piece.shape[0]

    def project_computed(rows):
        positions = jnp.arange(row_count, dtype=jnp.int32)
        query = jnp.dot(rows, w_query, preferred_element_type=jnp.float32).reshape(
            row_count, query_width // HD, HD
        )
        keyed = jnp.dot(rows, w_kv[0], preferred_element_type=jnp.float32).reshape(
            row_count, pair_width // HD, HD
        )
        valued = jnp.dot(rows, w_kv[1], preferred_element_type=jnp.float32)
        return jnp.concatenate(
            [
                rotate(query, positions).reshape(row_count, query_width),
                rotate(keyed, positions).reshape(row_count, pair_width),
                valued,
            ],
            axis=1,
        ).astype(jnp.bfloat16)

    def project_skipped(rows):
        return jnp.zeros((row_count, joined_width), jnp.bfloat16)

    joined = lax.cond(active, project_computed, project_skipped, piece)
    length = joined.shape[0]
    pair_heads = pair_width // HD
    group_size = query_width // pair_width

    def attend(joined_rows):
        query = joined_rows[:, :query_width].reshape(length, pair_heads, group_size, HD)
        keyed = joined_rows[:, query_width : query_width + pair_width].reshape(
            length, pair_heads, HD
        )
        valued = joined_rows[:, query_width + pair_width :].reshape(length, pair_heads, HD)
        scores = jnp.einsum(
            "qkgd,skd->kgqs", query, keyed, preferred_element_type=jnp.float32
        ) * HD ** (-0.5)
        row_ids = jnp.arange(length, dtype=jnp.int32)
        allowed = (segment_ids[:, None] == segment_ids[None, :]) & (
            row_ids[None, :] <= row_ids[:, None]
        )
        scores = jnp.where(allowed, scores, BLOCKED)
        probs = jax.nn.softmax(scores, axis=-1).astype(jnp.bfloat16)
        return (
            jnp.einsum("kgqs,skd->qkgd", probs, valued, preferred_element_type=jnp.float32)
            .astype(jnp.bfloat16)
            .reshape(length, query_width)
        )

    def attend_skipped(joined_rows):
        return jnp.zeros((length, query_width), jnp.bfloat16)

    mixed = lax.cond(active, attend, attend_skipped, joined)
    count = state.shape[0] * lax.axis_size("mp")

    def out_computed(values):
        return jnp.dot(values, w_out, preferred_element_type=jnp.float32)

    def out_skipped(values):
        return jnp.zeros((count, model_width), jnp.float32)

    summed = lax.psum_scatter(
        lax.cond(active, out_computed, out_skipped, mixed).astype(jnp.bfloat16),
        "mp",
        scatter_dimension=0,
        tiled=True,
    ).astype(jnp.float32)
    updated = (state.astype(jnp.float32) + summed).astype(jnp.bfloat16)
    return jnp.where(active, updated, state)


def shards(
    text,
    patches,
    segments,
    loss_mask,
    tile_batch,
    tile_offset,
    attn_gain,
    w_query,
    w_kv,
    w_out,
    vis_gain,
    vis_bias,
    v_qkv,
    v_out,
    v_up,
    v_down,
    v_proj,
):
    sections = lax.axis_size("section")
    section_at = lax.axis_index("section")
    part_at = lax.axis_index("mp")
    qkv_full, out_full, up_full, down_full, proj_full = one_gather(
        (v_qkv, v_out, v_up, v_down, v_proj), SECTION_DP, (1, 1, 0, 1, 0)
    )
    embedded = encode_tiles(
        patches, vis_gain, vis_bias, qkv_full, out_full, up_full, down_full, proj_full
    )
    length = segments.shape[2]
    tiles_here = embedded.shape[0] // POOL
    batch_all = tile_batch[0]
    offset_all = tile_offset[0]
    own_batch = lax.dynamic_slice_in_dim(batch_all, section_at * tiles_here, tiles_here, 0)
    capacity = tiles_here // 2
    block_rows = capacity * POOL
    local_ids = jnp.arange(tiles_here, dtype=jnp.int32)
    local_same = (own_batch[:, None] == own_batch[None, :]) & (
        local_ids[None, :] < local_ids[:, None]
    )
    local_rank = jnp.sum(local_same.astype(jnp.int32), axis=1)
    send_rows = jnp.arange(sections * block_rows, dtype=jnp.int32)
    send_target = send_rows // block_rows
    send_rank = send_rows % block_rows // POOL
    send_match = (own_batch[None, :] == send_target[:, None]) & (
        local_rank[None, :] == send_rank[:, None]
    )
    own_rows = jnp.arange(tiles_here * POOL, dtype=jnp.int32)
    send_pick = jnp.repeat(send_match, POOL, axis=1) & (
        (own_rows % POOL)[None, :] == (send_rows % POOL)[:, None]
    )
    blocks = jnp.dot(
        send_pick.astype(jnp.bfloat16), embedded, preferred_element_type=jnp.float32
    ).astype(jnp.bfloat16)
    arrived = lax.all_to_all(blocks, "section", split_axis=0, concat_axis=0, tiled=True)
    tile_ids = jnp.arange(batch_all.shape[0], dtype=jnp.int32)
    source_ids = tile_ids // tiles_here
    tile_same = (
        (batch_all[:, None] == batch_all[None, :])
        & (source_ids[:, None] == source_ids[None, :])
        & (tile_ids[None, :] < tile_ids[:, None])
    )
    tile_rank = jnp.sum(tile_same.astype(jnp.int32), axis=1)
    slot_rows = jnp.arange(sections * block_rows, dtype=jnp.int32)
    slot_source = slot_rows // block_rows
    slot_rank = slot_rows % block_rows // POOL
    match = (
        (batch_all[None, :] == section_at)
        & (source_ids[None, :] == slot_source[:, None])
        & (tile_rank[None, :] == slot_rank[:, None])
    )
    slot_place = jnp.sum(match.astype(jnp.int32) * offset_all[None, :], axis=1) + slot_rows % POOL
    slot_valid = jnp.any(match, axis=1)
    places = jnp.arange(length, dtype=jnp.int32)
    picker = ((places[:, None] == slot_place[None, :]) & slot_valid[None, :]).astype(jnp.bfloat16)
    image_cols = jnp.dot(picker, arrived, preferred_element_type=jnp.float32).astype(jnp.bfloat16)
    image_rows = lax.all_to_all(image_cols, "mp", split_axis=0, concat_axis=1, tiled=True)
    shard_rows = image_rows.shape[0]
    positions = part_at * shard_rows + jnp.arange(shard_rows, dtype=jnp.int32)
    covered = jnp.any(
        (batch_all[None, :] == section_at)
        & (positions[:, None] >= offset_all[None, :])
        & (positions[:, None] < offset_all[None, :] + POOL),
        axis=1,
    )
    start_state = jnp.where(covered[:, None], image_rows, text[0])
    gain_here = attn_gain[0]
    query_here = w_query[0]
    pair_here = w_kv[0]
    out_here = w_out[0]
    state = start_state
    segment_ids = segments[0, 0]
    for tick_index in range(2 * sections):
        if tick_index < 2 * sections - 1:
            micro_at = jnp.mod(section_at - tick_index, sections)
            begin_at = jnp.mod(sections - micro_at, sections)
            active = (tick_index >= begin_at) & (tick_index < begin_at + sections)
            state = decoder_layer(
                active, state, segment_ids, gain_here, query_here, pair_here, out_here
            )
        state, segment_ids = shifted((state, segment_ids), "section", 1)
    totals = over_axes(jnp.sum(loss_mask), SECTION_DP_MP)
    scaling = float(sections * lax.axis_size(DP) * length)
    token_weight = loss_mask.astype(jnp.float32) * scaling / totals.astype(jnp.float32)
    return (state[None], token_weight)


def solution(mesh):
    split = Mesh(
        mesh.devices.reshape(mesh.shape["section"], 4, 2, mesh.shape["mp"]),
        ("section", "dp_0", "dp_1", "mp"),
    )
    return jax.shard_map(
        shards,
        mesh=split,
        in_specs=(
            P("section", DP_MP, None),
            P(SECTION_DP, None),
            P("section", DP, None),
            P("section", DP_MP),
            P(DP, None),
            P(DP, None),
            P("section", None),
            P("section", None, "mp"),
            P("section", None, None, "mp"),
            P("section", "mp", None),
            P(),
            P(),
            P(None, SECTION_DP, "mp"),
            P("mp", SECTION_DP),
            P(SECTION_DP, "mp"),
            P("mp", SECTION_DP),
            P(SECTION_DP, "mp"),
        ),
        out_specs=(P("section", DP_MP, None), P("section", DP_MP)),
        check_vma=False,
    )
```

profile of v0, /device:TPU:32, one launch (start us, length us, event | category | flops | bytes accessed | tf_op | source)
XLA Modules:
  0.0 1387.6 jit_solution(4361427265575410445)
XLA Ops:
  16.4 66.2 %all-gather.24.cloned.1.call-done = bf16[7340032]{0:T(1024)(128)(2,1)} async-done(((bf16[229376]{0:T(1024)(128)(2,1)}), bf16[7340032]{0:T(1024)(128)(2,1)}) %all-gather.24.cloned.1.call-update) | async-done | bytes 14680080 | tf_op jit(solution)/shard_map/all_gather | solution.py:41
  141.0 27.2 %all-to-all-done = bf16[4,512,1024]{2,1,0:T(8,128)(2,1)} async-done(((bf16[4,512,1024]{2,1,0:T(8,128)(2,1)}), bf16[4,512,1024]{2,1,0:T(8,128)(2,1)}, u32[]{:S(2)}, u32[]{:S(2)}) %all-to-all-start) | async-done | bytes 4194336 | tf_op jit(solution)/shard_map/all_to_all | solution.py:25
  205.8 31.9 %all-to-all-done.1 = bf16[4,512,1024]{2,1,0:T(8,128)(2,1)} async-done(((bf16[4,512,1024]{2,1,0:T(8,128)(2,1)}), bf16[4,512,1024]{2,1,0:T(8,128)(2,1)}, u32[]{:S(2)}, u32[]{:S(2)}) %all-to-all-start.1) | async-done | bytes 4194336 | tf_op jit(solution)/shard_map/all_to_all | solution.py:25
  285.6 46.9 %all-gather.10.cloned.1.call-done = bf16[512,4096]{1,0:T(8,128)(2,1)} async-done(((bf16[128,4096]{1,0:T(8,128)(2,1)}), bf16[512,4096]{1,0:T(8,128)(2,1)}) %all-gather.10.cloned.1.call-update) | async-done | bytes 4194320 | tf_op jit(solution)/shard_map/all_gather | solution.py:144
  341.9 62.8 %reduce-scatter.8.cloned.1.call-done = bf16[128,4096]{1,0:T(8,128)(2,1)} async-done(((bf16[512,4096]{1,0:T(8,128)(2,1)}), bf16[128,4096]{1,0:T(8,128)(2,1)}) %reduce-scatter.8.cloned.1.call-update) | async-done | bytes 1048592 | tf_op jit(solution)/shard_map/reduce_scatter | solution.py:206
  435.0 46.4 %all-gather.12.cloned.1.call-done = bf16[512,4096]{1,0:T(8,128)(2,1)} async-done(((bf16[128,4096]{1,0:T(8,128)(2,1)}), bf16[512,4096]{1,0:T(8,128)(2,1)}) %all-gather.12.cloned.1.call-update) | async-done | bytes 4194320 | tf_op jit(solution)/shard_map/all_gather | solution.py:144
  509.2 45.7 %reduce-scatter.10.cloned.1.call-done = bf16[128,4096]{1,0:T(8,128)(2,1)} async-done(((bf16[512,4096]{1,0:T(8,128)(2,1)}), bf16[128,4096]{1,0:T(8,128)(2,1)}) %reduce-scatter.10.cloned.1.call-update) | async-done | bytes 1048592 | tf_op jit(solution)/shard_map/reduce_scatter | solution.py:206
  558.0 23.3 %collective-permute-done.2 = bf16[128,4096]{1,0:T(8,128)(2,1)S(1)} collective-permute-done((bf16[128,4096]{1,0:T(8,128)(2,1)S(1)}, bf16[128,4096]{1,0:T(8,128)(2,1)S(1)}, u32[]{:S(2)}, u32[]{:S(2)}) %collective-permute-start.2) | collective-permute-done | bytes 1048608 | tf_op jit(solution)/shard_map/ppermute | solution.py:52
  584.6 46.4 %all-gather.14.cloned.1.call-done = bf16[512,4096]{1,0:T(8,128)(2,1)} async-done(((bf16[128,4096]{1,0:T(8,128)(2,1)}), bf16[512,4096]{1,0:T(8,128)(2,1)}) %all-gather.14.cloned.1.call-update) | async-done | bytes 4194320 | tf_op jit(solution)/shard_map/all_gather | solution.py:144
  658.6 47.3 %reduce-scatter.12.cloned.1.call-done = bf16[128,4096]{1,0:T(8,128)(2,1)} async-done(((bf16[512,4096]{1,0:T(8,128)(2,1)}), bf16[128,4096]{1,0:T(8,128)(2,1)}) %reduce-scatter.12.cloned.1.call-update) | async-done | bytes 1048592 | tf_op jit(solution)/shard_map/reduce_scatter | solution.py:206
  709.0 23.3 %collective-permute-done.4 = bf16[128,4096]{1,0:T(8,128)(2,1)S(1)} collective-permute-done((bf16[128,4096]{1,0:T(8,128)(2,1)S(1)}, bf16[128,4096]{1,0:T(8,128)(2,1)S(1)}, u32[]{:S(2)}, u32[]{:S(2)}) %collective-permute-start.4) | collective-permute-done | bytes 1048608 | tf_op jit(solution)/shard_map/ppermute | solution.py:52
  735.6 46.4 %all-gather.16.cloned.1.call-done = bf16[512,4096]{1,0:T(8,128)(2,1)} async-done(((bf16[128,4096]{1,0:T(8,128)(2,1)}), bf16[512,4096]{1,0:T(8,128)(2,1)}) %all-gather.16.cloned.1.call-update) | async-done | bytes 4194320 | tf_op jit(solution)/shard_map/all_gather | solution.py:144
  810.0 46.8 %reduce-scatter.14.cloned.1.call-done = bf16[128,4096]{1,0:T(8,128)(2,1)} async-done(((bf16[512,4096]{1,0:T(8,128)(2,1)}), bf16[128,4096]{1,0:T(8,128)(2,1)}) %reduce-scatter.14.cloned.1.call-update) | async-done | bytes 1048592 | tf_op jit(solution)/shard_map/reduce_scatter | solution.py:206
  860.0 23.3 %collective-permute-done.6 = bf16[128,4096]{1,0:T(8,128)(2,1)S(1)} collective-permute-done((bf16[128,4096]{1,0:T(8,128)(2,1)S(1)}, bf16[128,4096]{1,0:T(8,128)(2,1)S(1)}, u32[]{:S(2)}, u32[]{:S(2)}) %collective-permute-start.6) | collective-permute-done | bytes 1048608 | tf_op jit(solution)/shard_map/ppermute | solution.py:52
  886.6 46.4 %all-gather.18.cloned.1.call-done = bf16[512,4096]{1,0:T(8,128)(2,1)} async-done(((bf16[128,4096]{1,0:T(8,128)(2,1)}), bf16[512,4096]{1,0:T(8,128)(2,1)}) %all-gather.18.cloned.1.call-update) | async-done | bytes 4194320 | tf_op jit(solution)/shard_map/all_gather | solution.py:144
  960.5 47.3 %reduce-scatter.16.cloned.1.call-done = bf16[128,4096]{1,0:T(8,128)(2,1)} async-done(((bf16[512,4096]{1,0:T(8,128)(2,1)}), bf16[128,4096]{1,0:T(8,128)(2,1)}) %reduce-scatter.16.cloned.1.call-update) | async-done | bytes 1048592 | tf_op jit(solution)/shard_map/reduce_scatter | solution.py:206
  1011.0 23.3 %collective-permute-done.8 = bf16[128,4096]{1,0:T(8,128)(2,1)S(1)} collective-permute-done((bf16[128,4096]{1,0:T(8,128)(2,1)S(1)}, bf16[128,4096]{1,0:T(8,128)(2,1)S(1)}, u32[]{:S(2)}, u32[]{:S(2)}) %collective-permute-start.8) | collective-permute-done | bytes 1048608 | tf_op jit(solution)/shard_map/ppermute | solution.py:52
  1037.5 46.4 %all-gather.20.cloned.1.call-done = bf16[512,4096]{1,0:T(8,128)(2,1)} async-done(((bf16[128,4096]{1,0:T(8,128)(2,1)}), bf16[512,4096]{1,0:T(8,128)(2,1)}) %all-gather.20.cloned.1.call-update) | async-done | bytes 4194320 | tf_op jit(solution)/shard_map/all_gather | solution.py:144
  1088.5 70.3 %reduce-scatter.18.cloned.1.call-done = bf16[128,4096]{1,0:T(8,128)(2,1)} async-done(((bf16[512,4096]{1,0:T(8,128)(2,1)}), bf16[128,4096]{1,0:T(8,128)(2,1)}) %reduce-scatter.18.cloned.1.call-update) | async-done | bytes 1048592 | tf_op jit(solution)/shard_map/reduce_scatter | solution.py:206
  1161.9 23.3 %collective-permute-done.10 = bf16[128,4096]{1,0:T(8,128)(2,1)S(1)} collective-permute-done((bf16[128,4096]{1,0:T(8,128)(2,1)S(1)}, bf16[128,4096]{1,0:T(8,128)(2,1)S(1)}, u32[]{:S(2)}, u32[]{:S(2)}) %collective-permute-start.10) | collective-permute-done | bytes 1048608 | tf_op jit(solution)/shard_map/ppermute | solution.py:52
  1188.5 46.4 %all-gather.22.cloned.1.call-done = bf16[512,4096]{1,0:T(8,128)(2,1)} async-done(((bf16[128,4096]{1,0:T(8,128)(2,1)}), bf16[512,4096]{1,0:T(8,128)(2,1)}) %all-gather.22.cloned.1.call-update) | async-done | bytes 4194320 | tf_op jit(solution)/shard_map/all_gather | solution.py:144
  1237.8 65.9 %reduce-scatter.20.cloned.1.call-done = bf16[128,4096]{1,0:T(8,128)(2,1)} async-done(((bf16[512,4096]{1,0:T(8,128)(2,1)}), bf16[128,4096]{1,0:T(8,128)(2,1)}) %reduce-scatter.20.cloned.1.call-update) | async-done | bytes 1048592 | tf_op jit(solution)/shard_map/reduce_scatter | solution.py:206
  1306.9 23.3 %collective-permute-done.12 = bf16[128,4096]{1,0:T(8,128)(2,1)S(1)} collective-permute-done((bf16[128,4096]{1,0:T(8,128)(2,1)S(1)}, bf16[128,4096]{1,0:T(8,128)(2,1)S(1)}, u32[]{:S(2)}, u32[]{:S(2)}) %collective-permute-start.12) | collective-permute-done | bytes 1048608 | tf_op jit(solution)/shard_map/ppermute | solution.py:52
  1332.3 26.3 %psum.28 = s32[]{:T(128)} all-reduce(s32[]{:T(128)} %reduce_sum.242), channel_id=1, replica_groups=mesh['section'=4,'dp_0'=4,'dp_1'=2,'mp'=4] {'section'}, use_global_device_ids=true, to_apply=%region_84.85 | all-reduce | flops 1 | bytes 8 | tf_op jit(solution)/shard_map/psum | solution.py:57
  (318 shorter events, 489.4 us)
Async XLA Ops:
  7.2 75.4 %all-gather.24.cloned.1.call-start = ((), (), s32[]{:S(2)}) async-start(), calls=%async_computation.25 | async-start | bytes 15138816 | tf_op jit(solution)/shard_map/all_gather | solution.py:41
  113.6 54.6 %all-to-all-start = ((bf16[4,512,1024]{2,1,0:T(8,128)(2,1)}), bf16[4,512,1024]{2,1,0:T(8,128)(2,1)}, u32[]{:S(2)}, u32[]{:S(2)}) async-start(bf16[4,512,1024]{2,1,0:T(8,128)(2,1)} %broadcast_in_dim.76), calls=%async_computation | async-start | bytes 8388608 | tf_op jit(solution)/shard_map/all_to_all | solution.py:25
  183.6 54.1 %all-to-all-start.1 = ((bf16[4,512,1024]{2,1,0:T(8,128)(2,1)}), bf16[4,512,1024]{2,1,0:T(8,128)(2,1)}, u32[]{:S(2)}, u32[]{:S(2)}) async-start(bf16[4,512,1024]{2,1,0:T(8,128)(2,1)} %broadcast_in_dim.85), calls=%async_computation.1 | async-start | bytes 8388608 | tf_op jit(solution)/shard_map/all_to_all | solution.py:25
  266.8 65.7 %all-gather.10.cloned.1.call-start = ((), (), s32[]{:S(2)}) async-start(), calls=%async_computation.11 | async-start | bytes 5242880 | tf_op jit(solution)/shard_map/all_gather | solution.py:144
  285.5 119.2 %reduce-scatter.8.cloned.1.call-start = ((), (), s32[]{:S(2)}) async-start(), calls=%async_computation.12 | async-start | bytes 5242880 | tf_op jit(solution)/shard_map/reduce_scatter | solution.py:206
  336.9 144.5 %all-gather.12.cloned.1.call-start = ((), (), s32[]{:S(2)}) async-start(), calls=%async_computation.13 | async-start | bytes 5242880 | tf_op jit(solution)/shard_map/all_gather | solution.py:144
  433.4 121.5 %reduce-scatter.10.cloned.1.call-start = ((), (), s32[]{:S(2)}) async-start(), calls=%async_computation.14 | async-start | bytes 5242880 | tf_op jit(solution)/shard_map/reduce_scatter | solution.py:206
  433.4 58.2 %collective-permute-start.1 = (s32[512]{0:T(512)S(1)}, s32[512]{0:T(512)S(1)}, u32[]{:S(2)}, u32[]{:S(2)}) collective-permute-start(s32[512]{0:T(512)S(1)} %bitcast.536), channel_id=1, source_target_pairs={{0,32},{32,64},{64,96},{96,0},{1,33},{33,65},{65,97},{97,1},{2,34}... | collective-permute-start | bytes 6152 | tf_op jit(solution)/shard_map/ppermute | solution.py:52
  509.2 121.9 %all-gather.14.cloned.1.call-start = ((), (), s32[]{:S(2)}) async-start(), calls=%async_computation.15 | async-start | bytes 5242880 | tf_op jit(solution)/shard_map/all_gather | solution.py:144
  583.0 122.9 %reduce-scatter.12.cloned.1.call-start = ((), (), s32[]{:S(2)}) async-start(), calls=%async_computation.16 | async-start | bytes 5242880 | tf_op jit(solution)/shard_map/reduce_scatter | solution.py:206
  583.0 58.2 %collective-permute-start.3 = (s32[512]{0:T(512)S(1)}, s32[512]{0:T(512)S(1)}, u32[]{:S(2)}, u32[]{:S(2)}) collective-permute-start(s32[512]{0:T(512)S(1)} %collective-permute-done.1), channel_id=1, source_target_pairs={{0,32},{32,64},{64,96},{96,0},{1,33},{33,65},{65,97},{97,1},{2,34}... | collective-permute-start | bytes 6152 | tf_op jit(solution)/shard_map/ppermute | solution.py:52
  658.5 123.4 %all-gather.16.cloned.1.call-start = ((), (), s32[]{:S(2)}) async-start(), calls=%async_computation.17 | async-start | bytes 5242880 | tf_op jit(solution)/shard_map/all_gather | solution.py:144
  733.9 122.9 %reduce-scatter.14.cloned.1.call-start = ((), (), s32[]{:S(2)}) async-start(), calls=%async_computation.18 | async-start | bytes 5242880 | tf_op jit(solution)/shard_map/reduce_scatter | solution.py:206
  733.9 58.4 %collective-permute-start.5 = (s32[512]{0:T(512)S(1)}, s32[512]{0:T(512)S(1)}, u32[]{:S(2)}, u32[]{:S(2)}) collective-permute-start(s32[512]{0:T(512)S(1)} %collective-permute-done.3), channel_id=1, source_target_pairs={{0,32},{32,64},{64,96},{96,0},{1,33},{33,65},{65,97},{97,1},{2,34}... | collective-permute-start | bytes 6152 | tf_op jit(solution)/shard_map/ppermute | solution.py:52
  809.5 123.4 %all-gather.18.cloned.1.call-start = ((), (), s32[]{:S(2)}) async-start(), calls=%async_computation.19 | async-start | bytes 5242880 | tf_op jit(solution)/shard_map/all_gather | solution.py:144
  884.9 122.9 %reduce-scatter.16.cloned.1.call-start = ((), (), s32[]{:S(2)}) async-start(), calls=%async_computation.20 | async-start | bytes 5242880 | tf_op jit(solution)/shard_map/reduce_scatter | solution.py:206
  884.9 58.2 %collective-permute-start.7 = (s32[512]{0:T(512)S(1)}, s32[512]{0:T(512)S(1)}, u32[]{:S(2)}, u32[]{:S(2)}) collective-permute-start(s32[512]{0:T(512)S(1)} %collective-permute-done.5), channel_id=1, source_target_pairs={{0,32},{32,64},{64,96},{96,0},{1,33},{33,65},{65,97},{97,1},{2,34}... | collective-permute-start | bytes 6152 | tf_op jit(solution)/shard_map/ppermute | solution.py:52
  960.5 123.4 %all-gather.20.cloned.1.call-start = ((), (), s32[]{:S(2)}) async-start(), calls=%async_computation.21 | async-start | bytes 5242880 | tf_op jit(solution)/shard_map/all_gather | solution.py:144
  1035.9 122.9 %reduce-scatter.18.cloned.1.call-start = ((), (), s32[]{:S(2)}) async-start(), calls=%async_computation.22 | async-start | bytes 5242880 | tf_op jit(solution)/shard_map/reduce_scatter | solution.py:206
  1035.9 48.9 %collective-permute-start.9 = (s32[512]{0:T(512)S(1)}, s32[512]{0:T(512)S(1)}, u32[]{:S(2)}, u32[]{:S(2)}) collective-permute-start(s32[512]{0:T(512)S(1)} %collective-permute-done.7), channel_id=1, source_target_pairs={{0,32},{32,64},{64,96},{96,0},{1,33},{33,65},{65,97},{97,1},{2,34}... | collective-permute-start | bytes 6152 | tf_op jit(solution)/shard_map/ppermute | solution.py:52
  1088.4 146.5 %all-gather.22.cloned.1.call-start = ((), (), s32[]{:S(2)}) async-start(), calls=%async_computation.23 | async-start | bytes 5242880 | tf_op jit(solution)/shard_map/all_gather | solution.py:144
  1186.8 116.9 %reduce-scatter.20.cloned.1.call-start = ((), (), s32[]{:S(2)}) async-start(), calls=%async_computation.24 | async-start | bytes 5242880 | tf_op jit(solution)/shard_map/reduce_scatter | solution.py:206
  1186.9 48.3 %collective-permute-start.11 = (s32[512]{0:T(512)S(1)}, s32[512]{0:T(512)S(1)}, u32[]{:S(2)}, u32[]{:S(2)}) collective-permute-start(s32[512]{0:T(512)S(1)} %collective-permute-done.9), channel_id=1, source_target_pairs={{0,32},{32,64},{64,96},{96,0},{1,33},{33,65},{65,97},{97,1},{2,34}... | collective-permute-start | bytes 6152 | tf_op jit(solution)/shard_map/ppermute | solution.py:52
  1330.1 49.6 %collective-permute-start.13 = (bf16[128,4096]{1,0:T(8,128)(2,1)S(1)}, bf16[128,4096]{1,0:T(8,128)(2,1)S(1)}, u32[]{:S(2)}, u32[]{:S(2)}) collective-permute-start(bf16[128,4096]{1,0:T(8,128)(2,1)S(1)} %collective-permute-done.12), channel_id=1, source_target_pairs={{0,32},{32,64},{64,96},{96,0},{1,33},{33,65},{65,97},{97,1},{2,34}... | collective-permute-start | bytes 3145736 | tf_op jit(solution)/shard_map/ppermute | solution.py:52
  (34 other events, 482.4 us)
Sparse Core Ops, SparseCore 0:
  13.2 69.3 all-gather.23
  285.6 46.8 all-gather.9
  337.1 67.6 reduce-scatter.7
  433.5 47.9 all-gather.11
  509.3 45.5 reduce-scatter.9
  583.1 47.8 all-gather.13
  658.6 47.1 reduce-scatter.11
  734.0 47.8 all-gather.15
  809.6 47.1 reduce-scatter.13
  885.0 47.9 all-gather.17
  960.6 47.1 reduce-scatter.15
  1036.0 47.8 all-gather.19
  1088.5 70.1 reduce-scatter.17
  1187.0 47.8 all-gather.21
  1237.9 65.7 reduce-scatter.19
where the time goes:
time: 1400 us; the launch traced here: 1390 us
  waiting for transfers between devices  1020 us (73%)
  local copies, waits for them, and re-layouts  106 us (8%)
  matrix products  101 us (7%)
  other arithmetic  51.4 us (4%)
  starting transfers between devices  48.4 us (3%)
  blocking collectives  46.2 us (3%)
  between operations  15.6 us (1%)
    reduce_scatter x7, waiting for transfers between devices, decoder_layer(): lax.psum_scatter(lax.cond(active, out_computed, out_skipped, mixed).astyp...  386 us
    all_gather x7, waiting for transfers between devices, decoder_layer(): piece = lax.all_gather(normed, 'mp', axis=0, tiled=True)  325 us
    ppermute x14, waiting for transfers between devices, shifted(): return lax.ppermute(value, axis, pairs)  163 us
    all_gather x1, waiting for transfers between devices, one_gather(): lines, at, done = (lax.all_gather(flat, axis), 0, [])  66.2 us
    all_to_all x2, waiting for transfers between devices, copy_for_each(): return lax.all_to_all(copies, axis, split_axis=0, concat_axis=0, tiled=True)  59.1 us
    psum x4, blocking collectives, over_axes(): array = lax.psum(array, axis)  46.2 us
  transfers between devices with their start and end apart: 33, of which 26 were waited for; matrix products, arithmetic and copies ran while one was open for 6% of the time, Pallas kernels for 0%

commit v1 on v0

v1 whole, which is shorter than its diff:
```python
import jax
import jax.numpy as jnp
from jax import lax
from jax.sharding import Mesh
from jax.sharding import PartitionSpec as P

HD = 128
VHD = 64
GRID = 16
PATCH = 256
POOL = 64
SECTION_DP = ("section", "dp_0", "dp_1")
MP_FIRST = ("mp", "section", "dp_0", "dp_1")
SECTION_DP_MP = ("section", "dp_0", "dp_1", "mp")
DP = ("dp_0", "dp_1")
DP_MP = ("dp_0", "dp_1", "mp")


EPS = 1e-05
ROPE_BASE = 500000.0
BLOCKED = -1e30


def dot(left, right):
    return jnp.dot(left, right, preferred_element_type=jnp.float32)


def exchange(blocks, axis):
    return lax.all_to_all(blocks, axis, split_axis=0, concat_axis=0, tiled=True)


def everywhere(array, axis):
    return exchange(jnp.broadcast_to(array, (lax.axis_size(axis), *array.shape)), axis)


def over_axes(array, axes):
    for axis in axes:
        array = lax.psum(array, axis)
    return array


def layer_norm(values, gain, bias):
    wide = values.astype(jnp.float32)
    center = wide - jnp.mean(wide, axis=-1, keepdims=True)
    spread = jnp.mean(center * center, axis=-1, keepdims=True)
    return (center * lax.rsqrt(spread + EPS) * gain + bias).astype(jnp.bfloat16)


def rms_norm(values, gain):
    wide = values.astype(jnp.float32)
    power = jnp.mean(wide * wide, axis=-1, keepdims=True)
    return (wide * lax.rsqrt(power + EPS) * gain).astype(jnp.bfloat16)


def rope_tables(length):
    half = HD // 2
    freqs = ROPE_BASE ** (-2.0 * jnp.arange(half, dtype=jnp.float32) / HD)
    angles = jnp.arange(length, dtype=jnp.float32)[:, None] * freqs[None, :]
    return jnp.cos(angles), jnp.sin(angles)


def rotate(values, cosine, sine):
    half = HD // 2
    first, second = values[:, :half], values[:, half:]
    return jnp.concatenate(
        [first * cosine - second * sine, second * cosine + first * sine], axis=1
    ).astype(jnp.bfloat16)


def pixel_shuffle(states):
    rows, width = states.shape
    side_half = GRID // 2
    arranged = states.reshape(rows // (2 * GRID), 2, side_half, 2, width)
    return arranged.transpose(0, 2, 1, 3, 4).reshape(rows // 4, 4 * width)


def summed_rows(partial):
    parts = lax.axis_size("mp")
    blocks = partial.astype(jnp.bfloat16).reshape(parts, -1, partial.shape[1])
    return jnp.sum(exchange(blocks, "mp").astype(jnp.float32), axis=0)


def encode_tiles(patches, vis_gain, vis_bias, slabs, part_at):
    up = slabs[:, 0:32].reshape(1024, 1024)
    down_t = slabs[:, 32:64].reshape(1024, 1024)
    proj = slabs[:, 64:192].reshape(4096, 1024)
    qkv = slabs[:, 192:224, :768].reshape(1024, 768)
    out_t = slabs[:, 192:224, 768:].reshape(1024, 256)
    tile_count = patches.shape[0] // PATCH
    local_width = qkv.shape[1] // 3
    head_count = local_width // VHD
    normed = layer_norm(patches, vis_gain[0], vis_bias[0])
    projected = dot(normed, qkv).astype(jnp.bfloat16)
    query, keyed, valued = (
        projected[:, i * local_width : (i + 1) * local_width].reshape(
            tile_count, PATCH, head_count, VHD
        )
        for i in range(3)
    )
    scores = jnp.einsum(
        "tqhd,tkhd->thqk", query, keyed, preferred_element_type=jnp.float32
    ) * VHD ** (-0.5)
    probs = jax.nn.softmax(scores, axis=-1).astype(jnp.bfloat16)
    mixed = (
        jnp.einsum("thqk,tkhd->tqhd", probs, valued, preferred_element_type=jnp.float32)
        .astype(jnp.bfloat16)
        .reshape(tile_count * PATCH, local_width)
    )
    contract_last = (((1,), (1,)), ((), ()))
    attended = summed_rows(
        lax.dot_general(mixed, out_t, contract_last, preferred_element_type=jnp.float32)
    )
    own_rows = attended.shape[0]
    own = lax.dynamic_slice_in_dim(patches, part_at * own_rows, own_rows, 0)
    residual = (own.astype(jnp.float32) + attended).astype(jnp.bfloat16)
    normed_two = everywhere(layer_norm(residual, vis_gain[1], vis_bias[1]), "mp").reshape(
        patches.shape
    )
    inner = jax.nn.gelu(dot(normed_two, up), approximate=False).astype(jnp.bfloat16)
    fed = summed_rows(
        lax.dot_general(inner, down_t, contract_last, preferred_element_type=jnp.float32)
    )
    states = (residual.astype(jnp.float32) + fed).astype(jnp.bfloat16)
    pooled = everywhere(pixel_shuffle(states), "mp").reshape(-1, 4 * states.shape[1])
    return dot(pooled, proj).astype(jnp.bfloat16)


def attend(state, allowed, cosine, sine, gain, w_joined):
    normed = rms_norm(state, gain)
    joined = dot(normed, w_joined)
    heads = w_joined.shape[1] // HD - 2
    keyed = rotate(joined[:, heads * HD : (heads + 1) * HD], cosine, sine)
    valued = joined[:, (heads + 1) * HD :].astype(jnp.bfloat16)
    mixes = []
    for head in range(heads):
        query = rotate(joined[:, head * HD : (head + 1) * HD], cosine, sine)
        scores = lax.dot_general(
            query, keyed, (((1,), (1,)), ((), ())), preferred_element_type=jnp.float32
        ) * HD ** (-0.5)
        scores = jnp.where(allowed, scores, BLOCKED)
        probs = jax.nn.softmax(scores, axis=-1).astype(jnp.bfloat16)
        mixes.append(dot(probs, valued).astype(jnp.bfloat16))
    return jnp.concatenate(mixes, axis=1)


def shards(
    text,
    patches,
    segments,
    loss_mask,
    tile_batch,
    tile_offset,
    attn_gain,
    w_query,
    w_kv,
    w_out,
    vis_gain,
    vis_bias,
    v_qkv,
    v_out,
    v_up,
    v_down,
    v_proj,
):
    sections = lax.axis_size("section")
    section_at = lax.axis_index("section")
    part_at = lax.axis_index("mp")
    dp_at = lax.axis_index(DP)
    dp_size = lax.axis_size(DP)
    length = segments.shape[2]

    qkv_rows = jnp.concatenate([v_qkv[0], v_qkv[1], v_qkv[2], v_out.T], axis=1)
    slab = jnp.concatenate([v_up, v_down.T, v_proj, qkv_rows], axis=0)
    slabs = lax.all_gather(slab, SECTION_DP)

    totals = over_axes(jnp.sum(loss_mask), SECTION_DP_MP)
    gains = lax.all_gather(attn_gain, "section", axis=0, tiled=True)
    own_out = w_out[0]
    rows_each = own_out.shape[0] // (sections * dp_size)
    out_blocks = own_out.reshape(sections, dp_size, rows_each, -1)
    out_blocks = lax.dynamic_index_in_dim(out_blocks, dp_at, 1, keepdims=False)
    out_blocks = exchange(out_blocks, "section")
    text_full = everywhere(text[0], "mp").reshape(length, -1)
    totals, gains, out_blocks, text_full, slabs, patches = lax.optimization_barrier(
        (totals, gains, out_blocks, text_full, slabs, patches)
    )

    depth = w_query.shape[1]
    rows = depth // dp_size
    q_own = lax.dynamic_slice_in_dim(w_query[0], dp_at * rows, rows, 0)
    kv_own = lax.dynamic_slice_in_dim(w_kv[0], dp_at * rows, rows, 1)
    joined_own = jnp.concatenate([q_own, kv_own[0], kv_own[1]], axis=1)
    joined_own, slabs = lax.optimization_barrier((joined_own, slabs))
    joined_all = lax.all_gather(joined_own, SECTION_DP, axis=0, tiled=True)
    joined_all = joined_all.reshape(sections, depth, -1)

    out_pairs = []
    half = sections // 2
    for pair in range(2):
        block = out_blocks[pair * half : (pair + 1) * half]
        out_pairs.append(lax.all_gather(block, MP_FIRST, axis=1, tiled=True))

    embedded = encode_tiles(patches, vis_gain, vis_bias, slabs, part_at)

    tiles_here = embedded.shape[0] // POOL
    batch_all = tile_batch[0]
    offset_all = tile_offset[0]
    own_batch = lax.dynamic_slice_in_dim(batch_all, section_at * tiles_here, tiles_here, 0)
    capacity = tiles_here // 2
    block_rows = capacity * POOL
    local_ids = jnp.arange(tiles_here, dtype=jnp.int32)
    local_same = (own_batch[:, None] == own_batch[None, :]) & (
        local_ids[None, :] < local_ids[:, None]
    )
    local_rank = jnp.sum(local_same.astype(jnp.int32), axis=1)
    send_rows = jnp.arange(sections * block_rows, dtype=jnp.int32)
    send_target = send_rows // block_rows
    send_rank = send_rows % block_rows // POOL
    send_match = (own_batch[None, :] == send_target[:, None]) & (
        local_rank[None, :] == send_rank[:, None]
    )
    own_rows = jnp.arange(tiles_here * POOL, dtype=jnp.int32)
    send_pick = jnp.repeat(send_match, POOL, axis=1) & (
        (own_rows % POOL)[None, :] == (send_rows % POOL)[:, None]
    )
    blocks = dot(send_pick.astype(jnp.bfloat16), embedded).astype(jnp.bfloat16)
    arrived = exchange(blocks, "section")
    arrived_all = everywhere(arrived, "mp")
    tile_ids = jnp.arange(batch_all.shape[0], dtype=jnp.int32)
    source_ids = tile_ids // tiles_here
    tile_same = (
        (batch_all[:, None] == batch_all[None, :])
        & (source_ids[:, None] == source_ids[None, :])
        & (tile_ids[None, :] < tile_ids[:, None])
    )
    tile_rank = jnp.sum(tile_same.astype(jnp.int32), axis=1)
    slot_rows = jnp.arange(sections * block_rows, dtype=jnp.int32)
    slot_source = slot_rows // block_rows
    slot_rank = slot_rows % block_rows // POOL
    match = (
        (batch_all[None, :] == section_at)
        & (source_ids[None, :] == slot_source[:, None])
        & (tile_rank[None, :] == slot_rank[:, None])
    )
    slot_place = jnp.sum(match.astype(jnp.int32) * offset_all[None, :], axis=1) + slot_rows % POOL
    slot_valid = jnp.any(match, axis=1)
    places = jnp.arange(length, dtype=jnp.int32)
    picker = ((places[:, None] == slot_place[None, :]) & slot_valid[None, :]).astype(jnp.bfloat16)
    covered = jnp.any(
        (batch_all[None, :] == section_at)
        & (places[:, None] >= offset_all[None, :])
        & (places[:, None] < offset_all[None, :] + POOL),
        axis=1,
    )
    image_rows = jnp.concatenate(
        [dot(picker, arrived_all[i]) for i in range(arrived_all.shape[0])], axis=1
    ).astype(jnp.bfloat16)
    state = jnp.where(covered[:, None], image_rows, text_full)

    segment_ids = segments[0, 0]
    allowed = (segment_ids[:, None] == segment_ids[None, :]) & (
        places[None, :] <= places[:, None]
    )
    cosine, sine = rope_tables(length)
    parts = lax.axis_size("mp")
    shard_rows = text.shape[1]
    for layer in range(sections):
        mixed = attend(state, allowed, cosine, sine, gains[layer], joined_all[layer])
        w_full = out_pairs[layer // half][layer % half]
        if layer == sections - 1:
            mine = exchange(mixed.reshape(parts, shard_rows, -1), "mp")
            state = lax.dynamic_slice_in_dim(state, part_at * shard_rows, shard_rows, 0)
        else:
            mine = everywhere(mixed, "mp")
        whole = jnp.concatenate([mine[i] for i in range(parts)], axis=1)
        state = (state.astype(jnp.float32) + dot(whole, w_full)).astype(jnp.bfloat16)

    scaling = float(sections * dp_size * length)
    token_weight = loss_mask.astype(jnp.float32) * scaling / totals.astype(jnp.float32)
    return (state[None], token_weight)


def solution(mesh):
    split = Mesh(
        mesh.devices.reshape(mesh.shape["section"], 4, 2, mesh.shape["mp"]),
        ("section", "dp_0", "dp_1", "mp"),
    )
    return jax.shard_map(
        shards,
        mesh=split,
        in_specs=(
            P("section", DP_MP, None),
            P(SECTION_DP, None),
            P("section", DP, None),
            P("section", DP_MP),
            P(DP, None),
            P(DP, None),
            P("section", None),
            P("section", None, "mp"),
            P("section", None, None, "mp"),
            P("section", "mp", None),
            P(),
            P(),
            P(None, SECTION_DP, "mp"),
            P("mp", SECTION_DP),
            P(SECTION_DP, "mp"),
            P("mp", SECTION_DP),
            P(SECTION_DP, "mp"),
        ),
        out_specs=(P("section", DP_MP, None), P("section", DP_MP)),
        check_vma=False,
    )
```

time: 1400 us -> 528 us (0.38)
  waiting for transfers between devices: 1020 us -> 101 us
  blocking collectives: 46.2 us -> 197 us
  local copies, waits for them, and re-layouts: 106 us -> 31.1 us
  other arithmetic: 51.4 us -> 25.5 us
  matrix products: 101 us -> 117 us
  starting transfers between devices: 48.4 us -> 32.8 us
    reduce_scatter x7 -> x0, waiting for transfers between devices: 386 us -> none  [decoder_layer(): lax.psum_scatter(lax.cond(active, out_computed, out_skipped, mixed).astyp...]
    all_gather x8 -> x4, waiting for transfers between devices: 391 us -> 35.8 us  [the longest x2 35.8 us: shards(): out_pairs.append(lax.all_gather(block, MP_FIRST, axis=1, tiled=True))]
    ppermute x14 -> x0, waiting for transfers between devices: 163 us -> none  [shifted(): return lax.ppermute(value, axis, pairs)]
    all_to_all x0 -> x4, blocking collectives: none -> 135 us  [exchange(): return lax.all_to_all(blocks, axis, split_axis=0, concat_axis=0, tiled=True)]
    another operation x15 -> x0, local copies, waits for them, and re-layouts: 31.6 us -> none
    ppermute x14 -> x0, starting transfers between devices: 22.7 us -> none  [shifted(): return lax.ppermute(value, axis, pairs)]
    dot_general x32 -> x49, matrix products: 98.9 us -> 115 us  [the longest x30 95.4 us: dot(): return jnp.dot(left, right, preferred_element_type=jnp.float32)]
    all_to_all x4 -> x8, starting transfers between devices: 19.8 us -> 32.6 us  [exchange(): return lax.all_to_all(blocks, axis, split_axis=0, concat_axis=0, tiled=True)]
  transfers between devices with their start and end apart: 33 -> 12, of which waited for: 26 -> 9; matrix products, arithmetic and copies ran while one was open for 6% -> 25% of each run, Pallas kernels for 0% -> 0%
where the time goes in v1:
time: 528 us; the launch traced here: 520 us
  blocking collectives  197 us (37%)
  matrix products  117 us (22%)
  waiting for transfers between devices  101 us (19%)
  starting transfers between devices  32.8 us (6%)
  local copies, waits for them, and re-layouts  31.1 us (6%)
  other arithmetic  25.5 us (5%)
  between operations  15.7 us (3%)
    all_to_all x4, blocking collectives, exchange(): return lax.all_to_all(blocks, axis, split_axis=0, concat_axis=0, tiled=True)  135 us
    dot_general x30, matrix products, dot(): return jnp.dot(left, right, preferred_element_type=jnp.float32)  95.4 us
    all_to_all x8, waiting for transfers between devices, exchange(): return lax.all_to_all(blocks, axis, split_axis=0, concat_axis=0, tiled=True)  64.6 us
    psum x4, blocking collectives, over_axes(): array = lax.psum(array, axis)  50.6 us
    all_gather x2, waiting for transfers between devices, shards(): out_pairs.append(lax.all_gather(block, MP_FIRST, axis=1, tiled=True))  35.8 us
    all_to_all x8, starting transfers between devices, exchange(): return lax.all_to_all(blocks, axis, split_axis=0, concat_axis=0, tiled=True)  32.6 us
    all_gather x1, blocking collectives, shards(): gains = lax.all_gather(attn_gain, 'section', axis=0, tiled=True)  11.2 us
  transfers between devices with their start and end apart: 12, of which 9 were waited for; matrix products, arithmetic and copies ran while one was open for 25% of the time, Pallas kernels for 0%

profile of v1, /device:TPU:32, one launch (start us, length us, event | category | flops | bytes accessed | tf_op | source)
XLA Modules:
  0.0 520.3 jit_solution(831585287304721016)
XLA Ops:
  10.9 13.2 %all_to_all.67 = bf16[4,16,4096]{2,1,0:T(8,128)(2,1)S(1)} all-to-all(bf16[4,16,4096]{2,1,0:T(8,128)(2,1)S(1)} %dynamic-slice_bitcast_fusion.1), channel_id=1, replica_groups=mesh['section'=4,'dp_0'=4,'dp_1'=2,'mp'=4] {'section'}, dimensions={0} | all-to-all | bytes 1048576 | tf_op jit(solution)/shard_map/all_to_all | solution.py:29
  32.5 7.9 %psum.28 = s32[]{:T(128)} all-reduce(s32[]{:T(128)} %reduce_sum.282), channel_id=1, replica_groups=mesh['section'=4,'dp_0'=4,'dp_1'=2,'mp'=4] {'section'}, use_global_device_ids=true, to_apply=%region_6.7 | all-reduce | flops 1 | bytes 8 | tf_op jit(solution)/shard_map/psum | solution.py:38
  40.5 9.8 %psum.29 = s32[]{:T(128)} all-reduce(s32[]{:T(128)} %psum.28), channel_id=1, replica_groups=mesh['section'=4,'dp_0'=4,'dp_1'=2,'mp'=4] {'dp_0'}, use_global_device_ids=true, to_apply=%region_7.8 | all-reduce | flops 1 | bytes 8 | tf_op jit(solution)/shard_map/psum | solution.py:38
  52.7 30.4 %psum.31 = s32[]{:T(128)} all-reduce(s32[]{:T(128)} %psum.30), channel_id=1, replica_groups=mesh['section'=4,'dp_0'=4,'dp_1'=2,'mp'=4] {'mp'}, use_global_device_ids=true, to_apply=%region_9.10 | all-reduce | flops 1 | bytes 8 | tf_op jit(solution)/shard_map/psum | solution.py:38
  83.1 11.2 %all-gather.1 = f32[4,1,4096]{2,1,0:T(1,128)S(1)} all-gather(f32[1,1,4096]{2,1,0:T(1,128)S(1)} %bitcast.189), channel_id=1, replica_groups=mesh['section'=4,'dp_0'=4,'dp_1'=2,'mp'=4] {'section'}, dimensions={0}, use_global_device_ids=true | all-gather | bytes 81920 | tf_op jit(solution)/shard_map/all_gather | solution.py:177
  114.0 10.9 %all-to-all-done.2 = bf16[4,128,1024]{2,1,0:T(8,128)(2,1)S(1)} async-done(((bf16[4,128,1024]{2,1,0:T(8,128)(2,1)}), bf16[4,128,1024]{2,1,0:T(8,128)(2,1)S(1)}, u32[]{:S(2)}, u32[]{:S(2)}) %all-to-all-start.2) | async-done | bytes 1048608 | tf_op jit(solution)/shard_map/all_to_all | solution.py:29
  134.8 6.6 %all-to-all-done.3 = bf16[4,128,1024]{2,1,0:T(8,128)(2,1)S(1)} async-done(((bf16[4,128,1024]{2,1,0:T(8,128)(2,1)}), bf16[4,128,1024]{2,1,0:T(8,128)(2,1)S(1)}, u32[]{:S(2)}, u32[]{:S(2)}) %all-to-all-start.3) | async-done | bytes 1048608 | tf_op jit(solution)/shard_map/all_to_all | solution.py:29
  141.4 8.9 %convolution_convert_fusion.4 = bf16[512,1024]{1,0:T(8,128)(2,1)} fusion(bf16[1024,1024]{1,0:T(8,128)(2,1)} %bitcast.175, bf16[512,1024]{1,0:T(8,128)(2,1)S(1)} %bitcast.180, bf16[1024,1024]{1,0:T(8,128)(2,1)S(1)} %bitcast.174), kind=kOutput, calls=%fused_computation.113 | convolution fusion | flops 2182086656 | bytes 6291456 | tf_op jit(solution)/shard_map/dot_general | solution.py:121
  153.8 10.8 %all-to-all-done.4 = bf16[4,128,1024]{2,1,0:T(8,128)(2,1)S(1)} async-done(((bf16[4,128,1024]{2,1,0:T(8,128)(2,1)}), bf16[4,128,1024]{2,1,0:T(8,128)(2,1)S(1)}, u32[]{:S(2)}, u32[]{:S(2)}) %all-to-all-start.4) | async-done | bytes 1048608 | tf_op jit(solution)/shard_map/all_to_all | solution.py:29
  170.5 8.5 %slice.371 = bf16[32,128,1024]{2,1,0:T(8,128)(2,1)} slice(bf16[32,224,1024]{2,1,0:T(8,128)(2,1)} %bitcast.170), slice={[0:32], [64:192], [0:1024]} | slice | bytes 16777216 | tf_op jit(solution)/shard_map/slice | solution.py:86
  204.8 19.1 %all-to-all-done.7 = bf16[4,256,1024]{2,1,0:T(8,128)(2,1)S(1)} async-done(((bf16[4,256,1024]{2,1,0:T(8,128)(2,1)}), bf16[4,256,1024]{2,1,0:T(8,128)(2,1)S(1)}, u32[]{:S(2)}, u32[]{:S(2)}) %all-to-all-start.7) | async-done | bytes 2097184 | tf_op jit(solution)/shard_map/all_to_all | solution.py:29
  231.0 7.4 %fusion.26 = f32[512,768]{1,0:T(8,128)S(1)} fusion(bf16[16384,768]{1,0:T(8,128)(2,1)} %all-gather.7.cloned.1.call-done, bf16[512,4096]{1,0:T(8,128)(2,1)} %get-tuple-element.19, f32[4096]{0:T(1024)S(1)} %bitcast.193, f32[512]{0:T(512)S(1)} %add_rsqrt_fusion.3), kind=kOutput, calls=%fused_computation.41 | convolution fusion | flops 3229614080 | bytes 12077056 | tf_op jit(solution)/shard_map/dot_general | solution.py:25
  245.4 33.1 %all_to_all.68 = bf16[4,512,512]{2,1,0:T(8,128)(2,1)S(1)} all-to-all(bf16[4,512,512]{2,1,0:T(8,128)(2,1)S(1)} %broadcast_in_dim.52), channel_id=1, replica_groups=mesh['section'=4,'dp_0'=4,'dp_1'=2,'mp'=4] {'mp'}, dimensions={0} | all-to-all | bytes 4194304 | tf_op jit(solution)/shard_map/all_to_all | solution.py:29
  278.6 34.5 %all-gather.9.cloned.1.call-done = bf16[2,2048,4096]{2,1,0:T(8,128)(2,1)} async-done(((bf16[2,16,4096]{2,1,0:T(8,128)(2,1)}), bf16[2,2048,4096]{2,1,0:T(8,128)(2,1)}) %all-gather.9.cloned.1.call-update) | async-done | bytes 33554448 | tf_op jit(solution)/shard_map/all_gather | solution.py:201
  313.1 13.3 %fusion.12 = (f32[512]{0:T(512)S(1)}, bf16[512,4096]{1,0:T(8,128)(2,1)S(1)}) fusion(bf16[2,2048,4096]{2,1,0:T(8,128)(2,1)} %all-gather.9.cloned.1.call-done, bf16[512,512]{1,0:T(8,128)(2,1)S(1)} %get-tuple-element.33, bf16[512,512]{1,0:T(8,128)(2,1)S(1)} %get-tuple-element.34, bf16[512,512]{1,0:T(8,128)(2,1)S(1)} %get-tuple-element.35, ...), kind=kOutput, calls=%fused_computation.27 | convolution fusion | flops 8610906112 | bytes 27265024 | tf_op jit(solution)/shard_map/dot_general | solution.py:25
  326.5 7.8 %fusion.24 = f32[512,768]{1,0:T(8,128)S(1)} fusion(bf16[16384,768]{1,0:T(8,128)(2,1)} %all-gather.7.cloned.1.call-done, bf16[512,4096]{1,0:T(8,128)(2,1)S(1)} %get-tuple-element.105, f32[4096]{0:T(1024)S(1)} %bitcast.192, f32[512]{0:T(512)S(1)} %add_rsqrt_fusion.2), kind=kOutput, calls=%fused_computation.39 | convolution fusion | flops 3229614080 | bytes 12077056 | tf_op jit(solution)/shard_map/dot_general | solution.py:25
  341.4 40.8 %all_to_all.69 = bf16[4,512,512]{2,1,0:T(8,128)(2,1)S(1)} all-to-all(bf16[4,512,512]{2,1,0:T(8,128)(2,1)S(1)} %broadcast_in_dim.53), channel_id=1, replica_groups=mesh['section'=4,'dp_0'=4,'dp_1'=2,'mp'=4] {'mp'}, dimensions={0} | all-to-all | bytes 4194304 | tf_op jit(solution)/shard_map/all_to_all | solution.py:29
  382.3 13.7 %fusion.16 = (f32[512]{0:T(512)S(1)}, bf16[512,4096]{1,0:T(8,128)(2,1)S(1)}) fusion(bf16[2,2048,4096]{2,1,0:T(8,128)(2,1)} %all-gather.9.cloned.1.call-done, bf16[512,512]{1,0:T(8,128)(2,1)S(1)} %get-tuple-element.29, bf16[512,512]{1,0:T(8,128)(2,1)S(1)} %get-tuple-element.30, bf16[512,512]{1,0:T(8,128)(2,1)S(1)} %get-tuple-element.31, ...), kind=kOutput, calls=%fused_computation.31 | convolution fusion | flops 8610906112 | bytes 27265024 | tf_op jit(solution)/shard_map/dot_general | solution.py:25
  396.1 8.0 %fusion.22 = f32[512,768]{1,0:T(8,128)S(1)} fusion(bf16[16384,768]{1,0:T(8,128)(2,1)} %all-gather.7.cloned.1.call-done, bf16[512,4096]{1,0:T(8,128)(2,1)S(1)} %get-tuple-element.115, f32[4096]{0:T(1024)S(1)} %bitcast.191, f32[512]{0:T(512)S(1)} %add_rsqrt_fusion.1), kind=kOutput, calls=%fused_computation.37 | convolution fusion | flops 3229614080 | bytes 12077056 | tf_op jit(solution)/shard_map/dot_general | solution.py:25
  411.2 48.2 %all_to_all.70 = bf16[4,512,512]{2,1,0:T(8,128)(2,1)S(1)} all-to-all(bf16[4,512,512]{2,1,0:T(8,128)(2,1)S(1)} %broadcast_in_dim.54), channel_id=1, replica_groups=mesh['section'=4,'dp_0'=4,'dp_1'=2,'mp'=4] {'mp'}, dimensions={0} | all-to-all | bytes 4194304 | tf_op jit(solution)/shard_map/all_to_all | solution.py:29
  460.8 13.3 %fusion.5 = (f32[512]{0:T(512)S(1)}, bf16[512,4096]{1,0:T(8,128)(2,1)S(1)}) fusion(bf16[2,2048,4096]{2,1,0:T(8,128)(2,1)} %all-gather.11.cloned.1.call-done, bf16[512,512]{1,0:T(8,128)(2,1)S(1)} %get-tuple-element.25, bf16[512,512]{1,0:T(8,128)(2,1)S(1)} %get-tuple-element.26, bf16[512,512]{1,0:T(8,128)(2,1)S(1)} %get-tuple-element.27, ...), kind=kOutput, calls=%fused_computation.20 | convolution fusion | flops 8610906112 | bytes 27265024 | tf_op jit(solution)/shard_map/dot_general | solution.py:25
  474.2 7.8 %fusion.20 = f32[512,768]{1,0:T(8,128)S(1)} fusion(bf16[16384,768]{1,0:T(8,128)(2,1)} %all-gather.7.cloned.1.call-done, bf16[512,4096]{1,0:T(8,128)(2,1)S(1)} %get-tuple-element.125, f32[4096]{0:T(1024)S(1)} %bitcast.190, f32[512]{0:T(512)S(1)} %add_rsqrt_fusion), kind=kOutput, calls=%fused_computation.35 | convolution fusion | flops 3229614080 | bytes 12077056 | tf_op jit(solution)/shard_map/dot_general | solution.py:25
  494.6 8.9 %all-to-all-done.11 = bf16[4,128,512]{2,1,0:T(8,128)(2,1)S(1)} async-done(((bf16[4,128,512]{2,1,0:T(8,128)(2,1)}), bf16[4,128,512]{2,1,0:T(8,128)(2,1)S(1)}, u32[]{:S(2)}, u32[]{:S(2)}) %all-to-all-start.11) | async-done | bytes 524320 | tf_op jit(solution)/shard_map/all_to_all | solution.py:29
  503.6 9.6 %fusion.30 = bf16[1,128,4096]{2,1,0:T(8,128)(2,1)} fusion(bf16[2,2048,4096]{2,1,0:T(8,128)(2,1)} %all-gather.11.cloned.1.call-done, bf16[512,4096]{1,0:T(8,128)(2,1)} %copy-done.10, s32[]{:T(128)S(6)} %select_n.152, bf16[128,512]{1,0:T(8,128)(2,1)S(1)} %get-tuple-element.78, bf16[128,512]{1,0:T(8,128)(2,1)S(1)} %get-tuple-element.79, ...), kind=kOutput, calls=%fused_computation.45 | convolution fusion | flops 2151153664 | bytes 19398660 | tf_op jit(solution)/shard_map/dot_general | solution.py:25
  (195 shorter events, 120.6 us)
Async XLA Ops:
  7.2 17.0 %copy-start.1 = (bf16[1,128,4096]{2,1,0:T(8,128)(2,1)S(1)}, bf16[1,128,4096]{2,1,0:T(8,128)(2,1)}, u32[]{:S(2)}) copy-start(bf16[1,128,4096]{2,1,0:T(8,128)(2,1)} %param.17) | copy-start | bytes 3145732
  7.2 90.3 %all-gather.13.cloned.1.call-start = ((), (), s32[]{:S(2)}) async-start(), calls=%async_computation.15 | async-start | bytes 15138816 | tf_op jit(solution)/shard_map/all_gather | solution.py:174
  26.8 5.1 copy-start.8
  26.8 56.3 %copy-start.2 = (f32[1,4096]{1,0:T(1,128)S(1)}, f32[1,4096]{1,0:T(1,128)}, u32[]{:S(2)}) copy-start(f32[1,4096]{1,0:T(1,128)} %param.23) | copy-start | bytes 49156
  26.8 70.7 %all-to-all-start.1 = ((bf16[4,128,4096]{2,1,0:T(8,128)(2,1)}), bf16[4,128,4096]{2,1,0:T(8,128)(2,1)}, u32[]{:S(2)}, u32[]{:S(2)}) async-start(bf16[4,128,4096]{2,1,0:T(8,128)(2,1)} %broadcast_in_dim.46), calls=%async_computation.1 | async-start | bytes 8388608 | tf_op jit(solution)/shard_map/all_to_all | solution.py:29
  31.8 199.1 %all-gather.7.cloned.1.call-start = ((), (), s32[]{:S(2)}) async-start(), calls=%async_computation.12 | async-start | bytes 25952256 | tf_op jit(solution)/shard_map/all_gather | solution.py:194
  96.5 2.6 copy-start.4
  97.5 215.6 %all-gather.9.cloned.1.call-start = ((), (), s32[]{:S(2)}) async-start(), calls=%async_computation.13 | async-start | bytes 33816576 | tf_op jit(solution)/shard_map/all_gather | solution.py:201
  98.5 362.4 %all-gather.11.cloned.1.call-start = ((), (), s32[]{:S(2)}) async-start(), calls=%async_computation.14 | async-start | bytes 33816576 | tf_op jit(solution)/shard_map/all_gather | solution.py:201
  99.1 2.7 copy-start
  110.5 14.4 %all-to-all-start.2 = ((bf16[4,128,1024]{2,1,0:T(8,128)(2,1)}), bf16[4,128,1024]{2,1,0:T(8,128)(2,1)S(1)}, u32[]{:S(2)}, u32[]{:S(2)}) async-start(bf16[4,128,1024]{2,1,0:T(8,128)(2,1)} %bitcast.25), calls=%async_computation.2 | async-start | bytes 2097152 | tf_op jit(solution)/shard_map/all_to_all | solution.py:29
  126.8 14.6 %all-to-all-start.3 = ((bf16[4,128,1024]{2,1,0:T(8,128)(2,1)}), bf16[4,128,1024]{2,1,0:T(8,128)(2,1)S(1)}, u32[]{:S(2)}, u32[]{:S(2)}) async-start(bf16[4,128,1024]{2,1,0:T(8,128)(2,1)} %broadcast_in_dim.48), calls=%async_computation.3 | async-start | bytes 2097152 | tf_op jit(solution)/shard_map/all_to_all | solution.py:29
  150.2 14.4 %all-to-all-start.4 = ((bf16[4,128,1024]{2,1,0:T(8,128)(2,1)}), bf16[4,128,1024]{2,1,0:T(8,128)(2,1)S(1)}, u32[]{:S(2)}, u32[]{:S(2)}) async-start(bf16[4,128,1024]{2,1,0:T(8,128)(2,1)} %bitcast.179), calls=%async_computation.4 | async-start | bytes 2097152 | tf_op jit(solution)/shard_map/all_to_all | solution.py:29
  165.2 4.8 copy-start.5
  166.5 14.4 %all-to-all-start.5 = ((bf16[4,32,4096]{2,1,0:T(8,128)(2,1)}), bf16[4,32,4096]{2,1,0:T(8,128)(2,1)S(1)}, u32[]{:S(2)}, u32[]{:S(2)}) async-start(bf16[4,32,4096]{2,1,0:T(8,128)(2,1)} %broadcast_in_dim.49), calls=%async_computation.5 | async-start | bytes 2097152 | tf_op jit(solution)/shard_map/all_to_all | solution.py:29
  180.9 11.5 %copy-start.6 = (s32[1,8]{1,0:T(1,128)S(1)}, s32[1,8]{1,0:T(1,128)}, u32[]{:S(2)}) copy-start(s32[1,8]{1,0:T(1,128)} %param.22) | copy-start | bytes 100
  186.7 12.1 %all-to-all-start.6 = ((bf16[4,64,1024]{2,1,0:T(8,128)(2,1)}), bf16[4,64,1024]{2,1,0:T(8,128)(2,1)S(1)}, u32[]{:S(2)}, u32[]{:S(2)}) async-start(bf16[4,64,1024]{2,1,0:T(8,128)(2,1)} %bitcast.35), calls=%async_computation.6 | async-start | bytes 1048576 | tf_op jit(solution)/shard_map/all_to_all | solution.py:29
  200.5 23.4 %all-to-all-start.7 = ((bf16[4,256,1024]{2,1,0:T(8,128)(2,1)}), bf16[4,256,1024]{2,1,0:T(8,128)(2,1)S(1)}, u32[]{:S(2)}, u32[]{:S(2)}) async-start(bf16[4,256,1024]{2,1,0:T(8,128)(2,1)} %broadcast_in_dim.50), calls=%async_computation.7 | async-start | bytes 4194304 | tf_op jit(solution)/shard_map/all_to_all | solution.py:29
  238.3 2.6 copy-start.7
  326.5 7.8 %copy-start.12 = (bf16[512,4096]{1,0:T(8,128)(2,1)}, bf16[512,4096]{1,0:T(8,128)(2,1)S(1)}, u32[]{:S(2)}) copy-start(bf16[512,4096]{1,0:T(8,128)(2,1)S(1)} %get-tuple-element.105) | copy-start | bytes 12582916
  396.1 8.0 %copy-start.11 = (bf16[512,4096]{1,0:T(8,128)(2,1)}, bf16[512,4096]{1,0:T(8,128)(2,1)S(1)}, u32[]{:S(2)}) copy-start(bf16[512,4096]{1,0:T(8,128)(2,1)S(1)} %get-tuple-element.115) | copy-start | bytes 12582916
  474.2 7.8 %copy-start.10 = (bf16[512,4096]{1,0:T(8,128)(2,1)}, bf16[512,4096]{1,0:T(8,128)(2,1)S(1)}, u32[]{:S(2)}) copy-start(bf16[512,4096]{1,0:T(8,128)(2,1)S(1)} %get-tuple-element.125) | copy-start | bytes 12582916
  488.6 5.5 %copy-start.9 = (s32[1,128]{1,0:T(1,128)S(1)}, s32[1,128]{1,0:T(1,128)}, u32[]{:S(2)}) copy-start(s32[1,128]{1,0:T(1,128)} %param.20) | copy-start | bytes 1540
  489.7 13.9 %all-to-all-start.11 = ((bf16[4,128,512]{2,1,0:T(8,128)(2,1)}), bf16[4,128,512]{2,1,0:T(8,128)(2,1)S(1)}, u32[]{:S(2)}, u32[]{:S(2)}) async-start(bf16[4,128,512]{2,1,0:T(8,128)(2,1)} %bitcast.61), calls=%async_computation.11 | async-start | bytes 1048576 | tf_op jit(solution)/shard_map/all_to_all | solution.py:29
  (1 other events, 2.6 us)
Sparse Core Ops, SparseCore 0:
  10.8 69.4 all-gather.12
  97.7 90.5 all-gather.6
  191.3 121.8 all-gather.8
  316.0 144.7 all-gather.10
